TPU v7x, 32 devices: a whole 2x2x4 slice. The times are simulated.
32 devices in a mesh: blk: 16 (over z, y, core), rows: 2 (over x).
Axes of the slice: x: 2, y: 2, z: 4, core: 2. Of those that a mesh axis runs over, the one named last changes fastest.
Arguments:
- columns: float32 [2048, 1280], P('blk', 'rows'), may hold values from -9 to 9
- right_factor: float32 [2048, 512], P('blk', 'rows'), may hold values from -6 to 6
Outputs:
- new_columns: float32 [2048, 1280], P('blk', 'rows')
- new_factor: float32 [2048, 512], P('blk', 'rows')
All inputs are finite; a program needn't handle non-finite values.
Results may differ from a plain program's by a relative error of at most 0.0003.
Values sent between devices are 32-bit elements; how exact they have to be, the bound alone decides.
A program may use at most 64 MiB of HBM per device.

v0:
```python
import jax
import jax.numpy as jnp
from jax import lax
from jax.sharding import PartitionSpec as P

STEPS = 6
HIGHEST_PREC = lax.Precision.HIGHEST


def shifted(block, axis, distance):
    devices = range(lax.axis_size(axis))
    route = [((i - distance) % len(devices), i) for i in devices]
    return lax.ppermute(block, axis, route)


def rotation(pair_gram):
    first = jnp.linalg.cholesky(jnp.dot(pair_gram, pair_gram, precision=HIGHEST_PREC))
    second = jnp.linalg.cholesky(jnp.dot(first.T, first, precision=HIGHEST_PREC))
    return jax.scipy.linalg.solve_triangular(second, first.T, lower=True).T


def gram_of(upper_rows, lower_rows):
    return lax.dot_general(upper_rows, lower_rows, (((1,), (1,)), ((), ())), precision=HIGHEST_PREC)


def rotate(rotation_matrix, blocks):
    return lax.dot_general(
        rotation_matrix, blocks, (((0,), (0,)), ((), ())), precision=HIGHEST_PREC
    )


def body(columns, right_factor):
    block_width = columns.shape[0] // 2
    stay_gram, moving_gram = lax.psum(
        (
            gram_of(columns[:block_width], columns[:block_width]),
            gram_of(columns[block_width:], columns[block_width:]),
        ),
        "rows",
    )

    def advance_cross(step_index, loop_state):
        column_pair, factor_pair, stay_gram, moving_gram = loop_state
        cross_term = lax.psum(gram_of(column_pair[:block_width], column_pair[block_width:]), "rows")
        upper_half = jnp.concatenate([stay_gram, cross_term], 1)
        lower_half = jnp.concatenate([cross_term.T, moving_gram], 1)
        pair_gram = jnp.concatenate([upper_half, lower_half], 0)
        rotation_matrix = rotation(pair_gram)
        column_pair = rotate(rotation_matrix, column_pair)
        factor_pair = rotate(rotation_matrix, factor_pair)
        rotated_gram = rotate(
            rotation_matrix, jnp.dot(pair_gram, rotation_matrix, precision=HIGHEST_PREC)
        )
        arrived = shifted(
            (
                column_pair[block_width:],
                factor_pair[block_width:],
                rotated_gram[block_width:, block_width:],
            ),
            "blk",
            1,
        )
        return (
            jnp.concatenate([column_pair[:block_width], arrived[0]], 0),
            jnp.concatenate([factor_pair[:block_width], arrived[1]], 0),
            rotated_gram[:block_width, :block_width],
            arrived[2],
        )

    result = lax.fori_loop(0, STEPS, advance_cross, (columns, right_factor, stay_gram, moving_gram))
    return (result[0], result[1])


def solution(mesh):
    return jax.shard_map(
        body,
        mesh=mesh,
        in_specs=(P("blk", "rows"), P("blk", "rows")),
        out_specs=(P("blk", "rows"), P("blk", "rows")),
        check_vma=False,
    )
```

profile of v0, /device:TPU:0, one launch (start us, length us, event | category | flops | bytes accessed | tf_op | source)
XLA Modules:
  0.0 344.3 jit_solution(13452265809952207676)
XLA Ops:
  2.2 10.4 %all-reduce = (f32[64,64]{1,0:T(8,128)S(1)}, f32[64,64]{1,0:T(8,128)S(1)}) all-reduce(f32[64,64]{1,0:T(8,128)S(1)} %fusion.27, f32[64,64]{1,0:T(8,128)S(1)} %fusion.25), channel_id=1, replica_groups=mesh['blk'=16,'rows'=2] {'rows'}, use_global_device_ids=true, to_apply=%region_0.0 | all-reduce | flops 8192 | bytes 65536 | tf_op jit(solution)/shard_map/psum | solution.py:34
  12.7 330.9 %while.16 = (s32[]{:T(128)}, f32[128,640]{1,0:T(8,128)S(1)}, f32[128,256]{1,0:T(8,128)S(1)}, f32[64,64]{1,0:T(8,128)S(1)}, f32[64,64]{1,0:T(8,128)S(1)}, /*index=5*/s32[]{:T(128)}) while((s32[]{:T(128)}, f32[128,640]{1,0:T(8,128)S(1)}, f32[128,256]{1,0:T(8,128)S(1)}, f32[64,64]{1,0:T(8,128)S(1)}, f32[64,64]{1,0:T(8,128)S(1)}, ...), condition=%wide.region_6.8_spmd, body=%wide.region_2.7_spmd.sunk | while | flops 333992192 | bytes 6179010 | solution.py:70
  13.2 6.9 %psum.24 = f32[64,64]{1,0:T(8,128)S(1)} all-reduce(f32[64,64]{1,0:T(8,128)S(1)} %fusion.77), channel_id=1, replica_groups=mesh['blk'=16,'rows'=2] {'rows'}, use_global_device_ids=true, to_apply=%region_3.0 | all-reduce | flops 4096 | bytes 32768 | tf_op jit(solution)/shard_map/while/body/eval_jaxpr/psum | solution.py:44
  20.7 11.7 %cholesky.175 = f32[128,128]{1,0:T(8,128)S(1)} custom-call(f32[128,128]{1,0:T(8,128)S(1)} %fusion.79), custom_call_target="Cholesky" | custom-call | tf_op jit(solution)/shard_map/while/body/eval_jaxpr/jit(cholesky)/cholesky | solution.py:17
  34.1 11.7 %cholesky.176 = f32[128,128]{1,0:T(8,128)S(1)} custom-call(f32[128,128]{1,0:T(8,128)S(1)} %fusion.82), custom_call_target="Cholesky" | custom-call | tf_op jit(solution)/shard_map/while/body/eval_jaxpr/jit(cholesky)/cholesky | solution.py:18
  47.3 9.8 %custom-call.7 = f32[1,128,128]{1,2,0:T(8,128)S(1)} custom-call(f32[1,128,128]{2,1,0:T(8,128)S(1)} %fusion.83), custom_call_target="InvertDiagBlocksLowerTriangular" | custom-call | tf_op jit(solution)/shard_map/while/body/eval_jaxpr/jit(_solve_triangular)/triangular_solve | solution.py:19
  61.5 3.2 collective-permute-done.1
  68.0 8.3 %psum.24 = f32[64,64]{1,0:T(8,128)S(1)} all-reduce(f32[64,64]{1,0:T(8,128)S(1)} %fusion.77), channel_id=1, replica_groups=mesh['blk'=16,'rows'=2] {'rows'}, use_global_device_ids=true, to_apply=%region_3.0 | all-reduce | flops 4096 | bytes 32768 | tf_op jit(solution)/shard_map/while/body/eval_jaxpr/psum | solution.py:44
  76.9 11.7 %cholesky.175 = f32[128,128]{1,0:T(8,128)S(1)} custom-call(f32[128,128]{1,0:T(8,128)S(1)} %fusion.79), custom_call_target="Cholesky" | custom-call | tf_op jit(solution)/shard_map/while/body/eval_jaxpr/jit(cholesky)/cholesky | solution.py:17
  90.4 11.7 %cholesky.176 = f32[128,128]{1,0:T(8,128)S(1)} custom-call(f32[128,128]{1,0:T(8,128)S(1)} %fusion.82), custom_call_target="Cholesky" | custom-call | tf_op jit(solution)/shard_map/while/body/eval_jaxpr/jit(cholesky)/cholesky | solution.py:18
  103.5 9.8 %custom-call.7 = f32[1,128,128]{1,2,0:T(8,128)S(1)} custom-call(f32[1,128,128]{2,1,0:T(8,128)S(1)} %fusion.83), custom_call_target="InvertDiagBlocksLowerTriangular" | custom-call | tf_op jit(solution)/shard_map/while/body/eval_jaxpr/jit(_solve_triangular)/triangular_solve | solution.py:19
  115.8 5.2 %collective-permute-done.1 = f32[64,256]{1,0:T(8,128)S(1)} collective-permute-done((f32[64,256]{1,0:T(8,128)S(1)}, f32[64,256]{1,0:T(8,128)S(1)}, u32[]{:S(2)}, u32[]{:S(2)}) %collective-permute-start.1) | collective-permute-done | bytes 65568 | tf_op jit(solution)/shard_map/while/body/eval_jaxpr/ppermute | solution.py:13
  123.6 7.4 %psum.24 = f32[64,64]{1,0:T(8,128)S(1)} all-reduce(f32[64,64]{1,0:T(8,128)S(1)} %fusion.77), channel_id=1, replica_groups=mesh['blk'=16,'rows'=2] {'rows'}, use_global_device_ids=true, to_apply=%region_3.0 | all-reduce | flops 4096 | bytes 32768 | tf_op jit(solution)/shard_map/while/body/eval_jaxpr/psum | solution.py:44
  131.6 11.7 %cholesky.175 = f32[128,128]{1,0:T(8,128)S(1)} custom-call(f32[128,128]{1,0:T(8,128)S(1)} %fusion.79), custom_call_target="Cholesky" | custom-call | tf_op jit(solution)/shard_map/while/body/eval_jaxpr/jit(cholesky)/cholesky | solution.py:17
  145.0 11.7 %cholesky.176 = f32[128,128]{1,0:T(8,128)S(1)} custom-call(f32[128,128]{1,0:T(8,128)S(1)} %fusion.82), custom_call_target="Cholesky" | custom-call | tf_op jit(solution)/shard_map/while/body/eval_jaxpr/jit(cholesky)/cholesky | solution.py:18
  158.2 9.8 %custom-call.7 = f32[1,128,128]{1,2,0:T(8,128)S(1)} custom-call(f32[1,128,128]{2,1,0:T(8,128)S(1)} %fusion.83), custom_call_target="InvertDiagBlocksLowerTriangular" | custom-call | tf_op jit(solution)/shard_map/while/body/eval_jaxpr/jit(_solve_triangular)/triangular_solve | solution.py:19
  170.5 5.2 %collective-permute-done.1 = f32[64,256]{1,0:T(8,128)S(1)} collective-permute-done((f32[64,256]{1,0:T(8,128)S(1)}, f32[64,256]{1,0:T(8,128)S(1)}, u32[]{:S(2)}, u32[]{:S(2)}) %collective-permute-start.1) | collective-permute-done | bytes 65568 | tf_op jit(solution)/shard_map/while/body/eval_jaxpr/ppermute | solution.py:13
  178.2 8.3 %psum.24 = f32[64,64]{1,0:T(8,128)S(1)} all-reduce(f32[64,64]{1,0:T(8,128)S(1)} %fusion.77), channel_id=1, replica_groups=mesh['blk'=16,'rows'=2] {'rows'}, use_global_device_ids=true, to_apply=%region_3.0 | all-reduce | flops 4096 | bytes 32768 | tf_op jit(solution)/shard_map/while/body/eval_jaxpr/psum | solution.py:44
  187.1 11.7 %cholesky.175 = f32[128,128]{1,0:T(8,128)S(1)} custom-call(f32[128,128]{1,0:T(8,128)S(1)} %fusion.79), custom_call_target="Cholesky" | custom-call | tf_op jit(solution)/shard_map/while/body/eval_jaxpr/jit(cholesky)/cholesky | solution.py:17
  200.6 11.7 %cholesky.176 = f32[128,128]{1,0:T(8,128)S(1)} custom-call(f32[128,128]{1,0:T(8,128)S(1)} %fusion.82), custom_call_target="Cholesky" | custom-call | tf_op jit(solution)/shard_map/while/body/eval_jaxpr/jit(cholesky)/cholesky | solution.py:18
  213.8 9.8 %custom-call.7 = f32[1,128,128]{1,2,0:T(8,128)S(1)} custom-call(f32[1,128,128]{2,1,0:T(8,128)S(1)} %fusion.83), custom_call_target="InvertDiagBlocksLowerTriangular" | custom-call | tf_op jit(solution)/shard_map/while/body/eval_jaxpr/jit(_solve_triangular)/triangular_solve | solution.py:19
  226.0 5.2 %collective-permute-done.1 = f32[64,256]{1,0:T(8,128)S(1)} collective-permute-done((f32[64,256]{1,0:T(8,128)S(1)}, f32[64,256]{1,0:T(8,128)S(1)}, u32[]{:S(2)}, u32[]{:S(2)}) %collective-permute-start.1) | collective-permute-done | bytes 65568 | tf_op jit(solution)/shard_map/while/body/eval_jaxpr/ppermute | solution.py:13
  233.8 7.4 %psum.24 = f32[64,64]{1,0:T(8,128)S(1)} all-reduce(f32[64,64]{1,0:T(8,128)S(1)} %fusion.77), channel_id=1, replica_groups=mesh['blk'=16,'rows'=2] {'rows'}, use_global_device_ids=true, to_apply=%region_3.0 | all-reduce | flops 4096 | bytes 32768 | tf_op jit(solution)/shard_map/while/body/eval_jaxpr/psum | solution.py:44
  241.8 11.7 %cholesky.175 = f32[128,128]{1,0:T(8,128)S(1)} custom-call(f32[128,128]{1,0:T(8,128)S(1)} %fusion.79), custom_call_target="Cholesky" | custom-call | tf_op jit(solution)/shard_map/while/body/eval_jaxpr/jit(cholesky)/cholesky | solution.py:17
  255.2 11.7 %cholesky.176 = f32[128,128]{1,0:T(8,128)S(1)} custom-call(f32[128,128]{1,0:T(8,128)S(1)} %fusion.82), custom_call_target="Cholesky" | custom-call | tf_op jit(solution)/shard_map/while/body/eval_jaxpr/jit(cholesky)/cholesky | solution.py:18
  268.4 9.8 %custom-call.7 = f32[1,128,128]{1,2,0:T(8,128)S(1)} custom-call(f32[1,128,128]{2,1,0:T(8,128)S(1)} %fusion.83), custom_call_target="InvertDiagBlocksLowerTriangular" | custom-call | tf_op jit(solution)/shard_map/while/body/eval_jaxpr/jit(_solve_triangular)/triangular_solve | solution.py:19
  280.7 5.2 %collective-permute-done.1 = f32[64,256]{1,0:T(8,128)S(1)} collective-permute-done((f32[64,256]{1,0:T(8,128)S(1)}, f32[64,256]{1,0:T(8,128)S(1)}, u32[]{:S(2)}, u32[]{:S(2)}) %collective-permute-start.1) | collective-permute-done | bytes 65568 | tf_op jit(solution)/shard_map/while/body/eval_jaxpr/ppermute | solution.py:13
  288.5 8.3 %psum.24 = f32[64,64]{1,0:T(8,128)S(1)} all-reduce(f32[64,64]{1,0:T(8,128)S(1)} %fusion.77), channel_id=1, replica_groups=mesh['blk'=16,'rows'=2] {'rows'}, use_global_device_ids=true, to_apply=%region_3.0 | all-reduce | flops 4096 | bytes 32768 | tf_op jit(solution)/shard_map/while/body/eval_jaxpr/psum | solution.py:44
  297.4 11.7 %cholesky.175 = f32[128,128]{1,0:T(8,128)S(1)} custom-call(f32[128,128]{1,0:T(8,128)S(1)} %fusion.79), custom_call_target="Cholesky" | custom-call | tf_op jit(solution)/shard_map/while/body/eval_jaxpr/jit(cholesky)/cholesky | solution.py:17
  310.8 11.7 %cholesky.176 = f32[128,128]{1,0:T(8,128)S(1)} custom-call(f32[128,128]{1,0:T(8,128)S(1)} %fusion.82), custom_call_target="Cholesky" | custom-call | tf_op jit(solution)/shard_map/while/body/eval_jaxpr/jit(cholesky)/cholesky | solution.py:18
  324.0 9.8 %custom-call.7 = f32[1,128,128]{1,2,0:T(8,128)S(1)} custom-call(f32[1,128,128]{2,1,0:T(8,128)S(1)} %fusion.83), custom_call_target="InvertDiagBlocksLowerTriangular" | custom-call | tf_op jit(solution)/shard_map/while/body/eval_jaxpr/jit(_solve_triangular)/triangular_solve | solution.py:19
  336.3 5.2 %collective-permute-done.1 = f32[64,256]{1,0:T(8,128)S(1)} collective-permute-done((f32[64,256]{1,0:T(8,128)S(1)}, f32[64,256]{1,0:T(8,128)S(1)}, u32[]{:S(2)}, u32[]{:S(2)}) %collective-permute-start.1) | collective-permute-done | bytes 65568 | tf_op jit(solution)/shard_map/while/body/eval_jaxpr/ppermute | solution.py:13
  (189 shorter events, 57.0 us)
Async XLA Ops:
  1.9 10.8 %copy-start.2 = (f32[128,256]{1,0:T(8,128)S(1)}, f32[128,256]{1,0:T(8,128)}, u32[]{:S(2)}) copy-start(f32[128,256]{1,0:T(8,128)} %param.6) | copy-start | bytes 393220
  58.3 6.4 %collective-permute-start.1 = (f32[64,256]{1,0:T(8,128)S(1)}, f32[64,256]{1,0:T(8,128)S(1)}, u32[]{:S(2)}, u32[]{:S(2)}) collective-permute-start(f32[64,256]{1,0:T(8,128)S(1)} %get-tuple-element.90), channel_id=1, source_target_pairs={{30,0},{0,2},{2,4},{4,6},{6,8},{8,10},{10,12},{12,14},{14,16},{16,... | collective-permute-start | bytes 196616 | tf_op jit(solution)/shard_map/while/body/eval_jaxpr/ppermute | solution.py:13
  58.8 7.7 %collective-permute-start = (f32[64,640]{1,0:T(8,128)S(1)}, f32[64,640]{1,0:T(8,128)S(1)}, u32[]{:S(2)}, u32[]{:S(2)}) collective-permute-start(f32[64,640]{1,0:T(8,128)S(1)} %get-tuple-element.88), channel_id=1, source_target_pairs={{30,0},{0,2},{2,4},{4,6},{6,8},{8,10},{10,12},{12,14},{14,16},{16,... | collective-permute-start | bytes 491528 | tf_op jit(solution)/shard_map/while/body/eval_jaxpr/ppermute | solution.py:13
  61.5 6.0 %collective-permute-start.2 = (f32[64,64]{1,0:T(8,128)S(1)}, f32[64,64]{1,0:T(8,128)S(1)}, u32[]{:S(2)}, u32[]{:S(2)}) collective-permute-start(f32[64,64]{1,0:T(8,128)S(1)} %get-tuple-element.93), channel_id=1, source_target_pairs={{30,0},{0,2},{2,4},{4,6},{6,8},{8,10},{10,12},{12,14},{14,16},{16,... | collective-permute-start | bytes 49160 | tf_op jit(solution)/shard_map/while/body/eval_jaxpr/ppermute | solution.py:13
  114.6 6.4 %collective-permute-start.1 = (f32[64,256]{1,0:T(8,128)S(1)}, f32[64,256]{1,0:T(8,128)S(1)}, u32[]{:S(2)}, u32[]{:S(2)}) collective-permute-start(f32[64,256]{1,0:T(8,128)S(1)} %get-tuple-element.90), channel_id=1, source_target_pairs={{30,0},{0,2},{2,4},{4,6},{6,8},{8,10},{10,12},{12,14},{14,16},{16,... | collective-permute-start | bytes 196616 | tf_op jit(solution)/shard_map/while/body/eval_jaxpr/ppermute | solution.py:13
  115.1 7.7 %collective-permute-start = (f32[64,640]{1,0:T(8,128)S(1)}, f32[64,640]{1,0:T(8,128)S(1)}, u32[]{:S(2)}, u32[]{:S(2)}) collective-permute-start(f32[64,640]{1,0:T(8,128)S(1)} %get-tuple-element.88), channel_id=1, source_target_pairs={{30,0},{0,2},{2,4},{4,6},{6,8},{8,10},{10,12},{12,14},{14,16},{16,... | collective-permute-start | bytes 491528 | tf_op jit(solution)/shard_map/while/body/eval_jaxpr/ppermute | solution.py:13
  115.8 7.3 %collective-permute-start.2 = (f32[64,64]{1,0:T(8,128)S(1)}, f32[64,64]{1,0:T(8,128)S(1)}, u32[]{:S(2)}, u32[]{:S(2)}) collective-permute-start(f32[64,64]{1,0:T(8,128)S(1)} %get-tuple-element.93), channel_id=1, source_target_pairs={{30,0},{0,2},{2,4},{4,6},{6,8},{8,10},{10,12},{12,14},{14,16},{16,... | collective-permute-start | bytes 49160 | tf_op jit(solution)/shard_map/while/body/eval_jaxpr/ppermute | solution.py:13
  169.2 6.4 %collective-permute-start.1 = (f32[64,256]{1,0:T(8,128)S(1)}, f32[64,256]{1,0:T(8,128)S(1)}, u32[]{:S(2)}, u32[]{:S(2)}) collective-permute-start(f32[64,256]{1,0:T(8,128)S(1)} %get-tuple-element.90), channel_id=1, source_target_pairs={{30,0},{0,2},{2,4},{4,6},{6,8},{8,10},{10,12},{12,14},{14,16},{16,... | collective-permute-start | bytes 196616 | tf_op jit(solution)/shard_map/while/body/eval_jaxpr/ppermute | solution.py:13
  169.7 7.7 %collective-permute-start = (f32[64,640]{1,0:T(8,128)S(1)}, f32[64,640]{1,0:T(8,128)S(1)}, u32[]{:S(2)}, u32[]{:S(2)}) collective-permute-start(f32[64,640]{1,0:T(8,128)S(1)} %get-tuple-element.88), channel_id=1, source_target_pairs={{30,0},{0,2},{2,4},{4,6},{6,8},{8,10},{10,12},{12,14},{14,16},{16,... | collective-permute-start | bytes 491528 | tf_op jit(solution)/shard_map/while/body/eval_jaxpr/ppermute | solution.py:13
  170.4 7.3 %collective-permute-start.2 = (f32[64,64]{1,0:T(8,128)S(1)}, f32[64,64]{1,0:T(8,128)S(1)}, u32[]{:S(2)}, u32[]{:S(2)}) collective-permute-start(f32[64,64]{1,0:T(8,128)S(1)} %get-tuple-element.93), channel_id=1, source_target_pairs={{30,0},{0,2},{2,4},{4,6},{6,8},{8,10},{10,12},{12,14},{14,16},{16,... | collective-permute-start | bytes 49160 | tf_op jit(solution)/shard_map/while/body/eval_jaxpr/ppermute | solution.py:13
  224.8 6.4 %collective-permute-start.1 = (f32[64,256]{1,0:T(8,128)S(1)}, f32[64,256]{1,0:T(8,128)S(1)}, u32[]{:S(2)}, u32[]{:S(2)}) collective-permute-start(f32[64,256]{1,0:T(8,128)S(1)} %get-tuple-element.90), channel_id=1, source_target_pairs={{30,0},{0,2},{2,4},{4,6},{6,8},{8,10},{10,12},{12,14},{14,16},{16,... | collective-permute-start | bytes 196616 | tf_op jit(solution)/shard_map/while/body/eval_jaxpr/ppermute | solution.py:13
  225.3 7.7 %collective-permute-start = (f32[64,640]{1,0:T(8,128)S(1)}, f32[64,640]{1,0:T(8,128)S(1)}, u32[]{:S(2)}, u32[]{:S(2)}) collective-permute-start(f32[64,640]{1,0:T(8,128)S(1)} %get-tuple-element.88), channel_id=1, source_target_pairs={{30,0},{0,2},{2,4},{4,6},{6,8},{8,10},{10,12},{12,14},{14,16},{16,... | collective-permute-start | bytes 491528 | tf_op jit(solution)/shard_map/while/body/eval_jaxpr/ppermute | solution.py:13
  226.0 7.3 %collective-permute-start.2 = (f32[64,64]{1,0:T(8,128)S(1)}, f32[64,64]{1,0:T(8,128)S(1)}, u32[]{:S(2)}, u32[]{:S(2)}) collective-permute-start(f32[64,64]{1,0:T(8,128)S(1)} %get-tuple-element.93), channel_id=1, source_target_pairs={{30,0},{0,2},{2,4},{4,6},{6,8},{8,10},{10,12},{12,14},{14,16},{16,... | collective-permute-start | bytes 49160 | tf_op jit(solution)/shard_map/while/body/eval_jaxpr/ppermute | solution.py:13
  279.4 6.4 %collective-permute-start.1 = (f32[64,256]{1,0:T(8,128)S(1)}, f32[64,256]{1,0:T(8,128)S(1)}, u32[]{:S(2)}, u32[]{:S(2)}) collective-permute-start(f32[64,256]{1,0:T(8,128)S(1)} %get-tuple-element.90), channel_id=1, source_target_pairs={{30,0},{0,2},{2,4},{4,6},{6,8},{8,10},{10,12},{12,14},{14,16},{16,... | collective-permute-start | bytes 196616 | tf_op jit(solution)/shard_map/while/body/eval_jaxpr/ppermute | solution.py:13
  280.0 7.7 %collective-permute-start = (f32[64,640]{1,0:T(8,128)S(1)}, f32[64,640]{1,0:T(8,128)S(1)}, u32[]{:S(2)}, u32[]{:S(2)}) collective-permute-start(f32[64,640]{1,0:T(8,128)S(1)} %get-tuple-element.88), channel_id=1, source_target_pairs={{30,0},{0,2},{2,4},{4,6},{6,8},{8,10},{10,12},{12,14},{14,16},{16,... | collective-permute-start | bytes 491528 | tf_op jit(solution)/shard_map/while/body/eval_jaxpr/ppermute | solution.py:13
  280.7 7.3 %collective-permute-start.2 = (f32[64,64]{1,0:T(8,128)S(1)}, f32[64,64]{1,0:T(8,128)S(1)}, u32[]{:S(2)}, u32[]{:S(2)}) collective-permute-start(f32[64,64]{1,0:T(8,128)S(1)} %get-tuple-element.93), channel_id=1, source_target_pairs={{30,0},{0,2},{2,4},{4,6},{6,8},{8,10},{10,12},{12,14},{14,16},{16,... | collective-permute-start | bytes 49160 | tf_op jit(solution)/shard_map/while/body/eval_jaxpr/ppermute | solution.py:13
  335.0 6.4 %collective-permute-start.1 = (f32[64,256]{1,0:T(8,128)S(1)}, f32[64,256]{1,0:T(8,128)S(1)}, u32[]{:S(2)}, u32[]{:S(2)}) collective-permute-start(f32[64,256]{1,0:T(8,128)S(1)} %get-tuple-element.90), channel_id=1, source_target_pairs={{30,0},{0,2},{2,4},{4,6},{6,8},{8,10},{10,12},{12,14},{14,16},{16,... | collective-permute-start | bytes 196616 | tf_op jit(solution)/shard_map/while/body/eval_jaxpr/ppermute | solution.py:13
  335.6 7.7 %collective-permute-start = (f32[64,640]{1,0:T(8,128)S(1)}, f32[64,640]{1,0:T(8,128)S(1)}, u32[]{:S(2)}, u32[]{:S(2)}) collective-permute-start(f32[64,640]{1,0:T(8,128)S(1)} %get-tuple-element.88), channel_id=1, source_target_pairs={{30,0},{0,2},{2,4},{4,6},{6,8},{8,10},{10,12},{12,14},{14,16},{16,... | collective-permute-start | bytes 491528 | tf_op jit(solution)/shard_map/while/body/eval_jaxpr/ppermute | solution.py:13
  336.3 7.3 %collective-permute-start.2 = (f32[64,64]{1,0:T(8,128)S(1)}, f32[64,64]{1,0:T(8,128)S(1)}, u32[]{:S(2)}, u32[]{:S(2)}) collective-permute-start(f32[64,64]{1,0:T(8,128)S(1)} %get-tuple-element.93), channel_id=1, source_target_pairs={{30,0},{0,2},{2,4},{4,6},{6,8},{8,10},{10,12},{12,14},{14,16},{16,... | collective-permute-start | bytes 49160 | tf_op jit(solution)/shard_map/while/body/eval_jaxpr/ppermute | solution.py:13
  343.6 0.7 copy-start
  343.6 0.8 copy-start.1
where the time goes:
time: 345 us; the launch traced here: 344 us
  other arithmetic  213 us (62%)
  blocking collectives  57.1 us (17%)
  waiting for transfers between devices  42.3 us (12%)
  matrix products  23.3 us (7%)
  local copies, waits for them, and re-layouts  4.8 us (1%)
    another operation x18, other arithmetic, rotation(): jnp.linalg.cholesky(jnp.dot(first.T, first, precision=HIGHEST_PREC))  74.8 us
    another operation x18, other arithmetic, rotation(): jnp.linalg.cholesky(jnp.dot(pair_gram, pair_gram, precision=HIGHEST_PREC))  74.3 us
    another operation x12, other arithmetic, rotation(): return jax.scipy.linalg.solve_triangular(second, first.T, lower=True).T  63.1 us
    psum x6, blocking collectives, advance_cross(): lax.psum(gram_of(column_pair[:block_width], column_pair[block_width:]), '...  46.7 us
    ppermute x18, waiting for transfers between devices, shifted(): return lax.ppermute(block, axis, route)  42.3 us
    psum x1, blocking collectives, body(): lax.psum((gram_of(columns[:block_width], columns[:block_width]), gram_of(...  10.4 us
  transfers between devices with their start and end apart: 18, of which 18 were waited for; matrix products, arithmetic and copies ran while one was open for 2% of the time, Pallas kernels for 0%

commit v1 on v0

--- a/solution.py
+++ b/solution.py
@@ -1,3 +1,4 @@
+import functools
 import jax
 import jax.numpy as jnp
 from jax import lax
@@ -5,6 +6,13 @@
 
 STEPS = 6
 HIGHEST_PREC = lax.Precision.HIGHEST
+
+
+def obtain_the_floor(v0, axis_key):
+    return jnp.sum(lax.all_gather(v0, axis_name=axis_key), axis=0)
+
+
+_detail_packet = functools.partial(obtain_the_floor, axis_key="rows")
 
 
 def shifted(block, axis, distance):
@@ -41,7 +49,7 @@
 
     def advance_cross(step_index, loop_state):
         column_pair, factor_pair, stay_gram, moving_gram = loop_state
-        cross_term = lax.psum(gram_of(column_pair[:block_width], column_pair[block_width:]), "rows")
+        cross_term = _detail_packet(gram_of(column_pair[:block_width], column_pair[block_width:]))
         upper_half = jnp.concatenate([stay_gram, cross_term], 1)
         lower_half = jnp.concatenate([cross_term.T, moving_gram], 1)
         pair_gram = jnp.concatenate([upper_half, lower_half], 0)

time: 345 us -> 324 us (0.939)
  blocking collectives: 57.1 us -> 37.9 us
    psum x6 -> x0, blocking collectives: 46.7 us -> none  [advance_cross(): lax.psum(gram_of(column_pair[:block_width], column_pair[block_width:]), '...]
    all_gather x0 -> x6, blocking collectives: none -> 27.5 us  [obtain_the_floor(): return jnp.sum(lax.all_gather(v0, axis_name=axis_key), axis=0)]
where the time goes in v1:
time: 324 us; the launch traced here: 323 us
  other arithmetic  213 us (66%)
  waiting for transfers between devices  42.5 us (13%)
  blocking collectives  37.9 us (12%)
  matrix products  22.4 us (7%)
  local copies, waits for them, and re-layouts  3.9 us (1%)
    another operation x18, other arithmetic, rotation(): jnp.linalg.cholesky(jnp.dot(first.T, first, precision=HIGHEST_PREC))  74.8 us
    another operation x18, other arithmetic, rotation(): jnp.linalg.cholesky(jnp.dot(pair_gram, pair_gram, precision=HIGHEST_PREC))  74.3 us
    another operation x12, other arithmetic, rotation(): return jax.scipy.linalg.solve_triangular(second, first.T, lower=True).T  63.1 us
    ppermute x18, waiting for transfers between devices, shifted(): return lax.ppermute(block, axis, route)  42.5 us
    all_gather x6, blocking collectives, obtain_the_floor(): return jnp.sum(lax.all_gather(v0, axis_name=axis_key), axis=0)  27.5 us
    psum x1, blocking collectives, body(): lax.psum((gram_of(columns[:block_width], columns[:block_width]), gram_of(...  10.4 us
  transfers between devices with their start and end apart: 18, of which 18 were waited for; matrix products, arithmetic and copies ran while one was open for 2% of the time, Pallas kernels for 0%

profile of v1, /device:TPU:0, one launch (start us, length us, event | category | flops | bytes accessed | tf_op | source)
XLA Modules:
  0.0 323.2 jit_solution(8555355982239525635)
XLA Ops:
  2.2 10.4 %all-reduce = (f32[64,64]{1,0:T(8,128)S(1)}, f32[64,64]{1,0:T(8,128)S(1)}) all-reduce(f32[64,64]{1,0:T(8,128)S(1)} %fusion.27, f32[64,64]{1,0:T(8,128)S(1)} %fusion.25), channel_id=1, replica_groups=mesh['blk'=16,'rows'=2] {'rows'}, use_global_device_ids=true, to_apply=%region_0.0 | all-reduce | flops 8192 | bytes 65536 | tf_op jit(solution)/shard_map/psum | solution.py:42
  12.7 309.7 %while.16 = (s32[]{:T(128)}, f32[128,640]{1,0:T(8,128)S(1)}, f32[128,256]{1,0:T(8,128)S(1)}, f32[64,64]{1,0:T(8,128)S(1)}, f32[64,64]{1,0:T(8,128)S(1)}, /*index=5*/s32[]{:T(128)}, f32[]{:T(128)}) while((s32[]{:T(128)}, f32[128,640]{1,0:T(8,128)S(1)}, f32[128,256]{1,0:T(8,128)S(1)}, f32[64,64]{1,0:T(8,128)S(1)}, f32[64,64]{1,0:T(8,128)S(1)}, ...), condition=%wide.region_6.8_spmd, body=%wide.region_2.7_spmd.sunk | while | flops 333992192 | bytes 6179022 | solution.py:78
  13.0 4.6 %all-gather.2 = f32[128,64]{1,0:T(8,128)S(1)} all-gather(f32[64,64]{1,0:T(8,128)S(1)} %fusion.77), channel_id=2, replica_groups=mesh['blk'=16,'rows'=2] {'rows'}, dimensions={0}, use_global_device_ids=true | all-gather | bytes 49152 | tf_op jit(solution)/shard_map/while/body/eval_jaxpr/all_gather | solution.py:12
  18.1 11.7 %cholesky.175 = f32[128,128]{1,0:T(8,128)S(1)} custom-call(f32[128,128]{1,0:T(8,128)S(1)} %fusion.79), custom_call_target="Cholesky" | custom-call | tf_op jit(solution)/shard_map/while/body/eval_jaxpr/jit(cholesky)/cholesky | solution.py:25
  31.5 11.7 %cholesky.176 = f32[128,128]{1,0:T(8,128)S(1)} custom-call(f32[128,128]{1,0:T(8,128)S(1)} %fusion.82), custom_call_target="Cholesky" | custom-call | tf_op jit(solution)/shard_map/while/body/eval_jaxpr/jit(cholesky)/cholesky | solution.py:26
  44.7 9.8 %custom-call.7 = f32[1,128,128]{1,2,0:T(8,128)S(1)} custom-call(f32[1,128,128]{2,1,0:T(8,128)S(1)} %fusion.83), custom_call_target="InvertDiagBlocksLowerTriangular" | custom-call | tf_op jit(solution)/shard_map/while/body/eval_jaxpr/jit(_solve_triangular)/triangular_solve | solution.py:27
  58.4 3.8 %collective-permute-done.1 = f32[64,256]{1,0:T(8,128)S(1)} collective-permute-done((f32[64,256]{1,0:T(8,128)S(1)}, f32[64,256]{1,0:T(8,128)S(1)}, u32[]{:S(2)}, u32[]{:S(2)}) %collective-permute-start.1) | collective-permute-done | bytes 65568 | tf_op jit(solution)/shard_map/while/body/eval_jaxpr/ppermute | solution.py:21
  64.7 4.6 %all-gather.2 = f32[128,64]{1,0:T(8,128)S(1)} all-gather(f32[64,64]{1,0:T(8,128)S(1)} %fusion.77), channel_id=2, replica_groups=mesh['blk'=16,'rows'=2] {'rows'}, dimensions={0}, use_global_device_ids=true | all-gather | bytes 49152 | tf_op jit(solution)/shard_map/while/body/eval_jaxpr/all_gather | solution.py:12
  69.8 11.7 %cholesky.175 = f32[128,128]{1,0:T(8,128)S(1)} custom-call(f32[128,128]{1,0:T(8,128)S(1)} %fusion.79), custom_call_target="Cholesky" | custom-call | tf_op jit(solution)/shard_map/while/body/eval_jaxpr/jit(cholesky)/cholesky | solution.py:25
  83.3 11.7 %cholesky.176 = f32[128,128]{1,0:T(8,128)S(1)} custom-call(f32[128,128]{1,0:T(8,128)S(1)} %fusion.82), custom_call_target="Cholesky" | custom-call | tf_op jit(solution)/shard_map/while/body/eval_jaxpr/jit(cholesky)/cholesky | solution.py:26
  96.4 9.8 %custom-call.7 = f32[1,128,128]{1,2,0:T(8,128)S(1)} custom-call(f32[1,128,128]{2,1,0:T(8,128)S(1)} %fusion.83), custom_call_target="InvertDiagBlocksLowerTriangular" | custom-call | tf_op jit(solution)/shard_map/while/body/eval_jaxpr/jit(_solve_triangular)/triangular_solve | solution.py:27
  108.7 5.2 %collective-permute-done.1 = f32[64,256]{1,0:T(8,128)S(1)} collective-permute-done((f32[64,256]{1,0:T(8,128)S(1)}, f32[64,256]{1,0:T(8,128)S(1)}, u32[]{:S(2)}, u32[]{:S(2)}) %collective-permute-start.1) | collective-permute-done | bytes 65568 | tf_op jit(solution)/shard_map/while/body/eval_jaxpr/ppermute | solution.py:21
  116.3 4.6 %all-gather.2 = f32[128,64]{1,0:T(8,128)S(1)} all-gather(f32[64,64]{1,0:T(8,128)S(1)} %fusion.77), channel_id=2, replica_groups=mesh['blk'=16,'rows'=2] {'rows'}, dimensions={0}, use_global_device_ids=true | all-gather | bytes 49152 | tf_op jit(solution)/shard_map/while/body/eval_jaxpr/all_gather | solution.py:12
  121.4 11.7 %cholesky.175 = f32[128,128]{1,0:T(8,128)S(1)} custom-call(f32[128,128]{1,0:T(8,128)S(1)} %fusion.79), custom_call_target="Cholesky" | custom-call | tf_op jit(solution)/shard_map/while/body/eval_jaxpr/jit(cholesky)/cholesky | solution.py:25
  134.9 11.7 %cholesky.176 = f32[128,128]{1,0:T(8,128)S(1)} custom-call(f32[128,128]{1,0:T(8,128)S(1)} %fusion.82), custom_call_target="Cholesky" | custom-call | tf_op jit(solution)/shard_map/while/body/eval_jaxpr/jit(cholesky)/cholesky | solution.py:26
  148.0 9.8 %custom-call.7 = f32[1,128,128]{1,2,0:T(8,128)S(1)} custom-call(f32[1,128,128]{2,1,0:T(8,128)S(1)} %fusion.83), custom_call_target="InvertDiagBlocksLowerTriangular" | custom-call | tf_op jit(solution)/shard_map/while/body/eval_jaxpr/jit(_solve_triangular)/triangular_solve | solution.py:27
  160.3 5.2 %collective-permute-done.1 = f32[64,256]{1,0:T(8,128)S(1)} collective-permute-done((f32[64,256]{1,0:T(8,128)S(1)}, f32[64,256]{1,0:T(8,128)S(1)}, u32[]{:S(2)}, u32[]{:S(2)}) %collective-permute-start.1) | collective-permute-done | bytes 65568 | tf_op jit(solution)/shard_map/while/body/eval_jaxpr/ppermute | solution.py:21
  167.9 4.6 %all-gather.2 = f32[128,64]{1,0:T(8,128)S(1)} all-gather(f32[64,64]{1,0:T(8,128)S(1)} %fusion.77), channel_id=2, replica_groups=mesh['blk'=16,'rows'=2] {'rows'}, dimensions={0}, use_global_device_ids=true | all-gather | bytes 49152 | tf_op jit(solution)/shard_map/while/body/eval_jaxpr/all_gather | solution.py:12
  173.0 11.7 %cholesky.175 = f32[128,128]{1,0:T(8,128)S(1)} custom-call(f32[128,128]{1,0:T(8,128)S(1)} %fusion.79), custom_call_target="Cholesky" | custom-call | tf_op jit(solution)/shard_map/while/body/eval_jaxpr/jit(cholesky)/cholesky | solution.py:25
  186.4 11.7 %cholesky.176 = f32[128,128]{1,0:T(8,128)S(1)} custom-call(f32[128,128]{1,0:T(8,128)S(1)} %fusion.82), custom_call_target="Cholesky" | custom-call | tf_op jit(solution)/shard_map/while/body/eval_jaxpr/jit(cholesky)/cholesky | solution.py:26
  199.6 9.8 %custom-call.7 = f32[1,128,128]{1,2,0:T(8,128)S(1)} custom-call(f32[1,128,128]{2,1,0:T(8,128)S(1)} %fusion.83), custom_call_target="InvertDiagBlocksLowerTriangular" | custom-call | tf_op jit(solution)/shard_map/while/body/eval_jaxpr/jit(_solve_triangular)/triangular_solve | solution.py:27
  211.9 5.2 %collective-permute-done.1 = f32[64,256]{1,0:T(8,128)S(1)} collective-permute-done((f32[64,256]{1,0:T(8,128)S(1)}, f32[64,256]{1,0:T(8,128)S(1)}, u32[]{:S(2)}, u32[]{:S(2)}) %collective-permute-start.1) | collective-permute-done | bytes 65568 | tf_op jit(solution)/shard_map/while/body/eval_jaxpr/ppermute | solution.py:21
  219.5 4.6 %all-gather.2 = f32[128,64]{1,0:T(8,128)S(1)} all-gather(f32[64,64]{1,0:T(8,128)S(1)} %fusion.77), channel_id=2, replica_groups=mesh['blk'=16,'rows'=2] {'rows'}, dimensions={0}, use_global_device_ids=true | all-gather | bytes 49152 | tf_op jit(solution)/shard_map/while/body/eval_jaxpr/all_gather | solution.py:12
  224.6 11.7 %cholesky.175 = f32[128,128]{1,0:T(8,128)S(1)} custom-call(f32[128,128]{1,0:T(8,128)S(1)} %fusion.79), custom_call_target="Cholesky" | custom-call | tf_op jit(solution)/shard_map/while/body/eval_jaxpr/jit(cholesky)/cholesky | solution.py:25
  238.0 11.7 %cholesky.176 = f32[128,128]{1,0:T(8,128)S(1)} custom-call(f32[128,128]{1,0:T(8,128)S(1)} %fusion.82), custom_call_target="Cholesky" | custom-call | tf_op jit(solution)/shard_map/while/body/eval_jaxpr/jit(cholesky)/cholesky | solution.py:26
  251.2 9.8 %custom-call.7 = f32[1,128,128]{1,2,0:T(8,128)S(1)} custom-call(f32[1,128,128]{2,1,0:T(8,128)S(1)} %fusion.83), custom_call_target="InvertDiagBlocksLowerTriangular" | custom-call | tf_op jit(solution)/shard_map/while/body/eval_jaxpr/jit(_solve_triangular)/triangular_solve | solution.py:27
  263.5 5.2 %collective-permute-done.1 = f32[64,256]{1,0:T(8,128)S(1)} collective-permute-done((f32[64,256]{1,0:T(8,128)S(1)}, f32[64,256]{1,0:T(8,128)S(1)}, u32[]{:S(2)}, u32[]{:S(2)}) %collective-permute-start.1) | collective-permute-done | bytes 65568 | tf_op jit(solution)/shard_map/while/body/eval_jaxpr/ppermute | solution.py:21
  271.1 4.6 %all-gather.2 = f32[128,64]{1,0:T(8,128)S(1)} all-gather(f32[64,64]{1,0:T(8,128)S(1)} %fusion.77), channel_id=2, replica_groups=mesh['blk'=16,'rows'=2] {'rows'}, dimensions={0}, use_global_device_ids=true | all-gather | bytes 49152 | tf_op jit(solution)/shard_map/while/body/eval_jaxpr/all_gather | solution.py:12
  276.2 11.7 %cholesky.175 = f32[128,128]{1,0:T(8,128)S(1)} custom-call(f32[128,128]{1,0:T(8,128)S(1)} %fusion.79), custom_call_target="Cholesky" | custom-call | tf_op jit(solution)/shard_map/while/body/eval_jaxpr/jit(cholesky)/cholesky | solution.py:25
  289.6 11.7 %cholesky.176 = f32[128,128]{1,0:T(8,128)S(1)} custom-call(f32[128,128]{1,0:T(8,128)S(1)} %fusion.82), custom_call_target="Cholesky" | custom-call | tf_op jit(solution)/shard_map/while/body/eval_jaxpr/jit(cholesky)/cholesky | solution.py:26
  302.8 9.8 %custom-call.7 = f32[1,128,128]{1,2,0:T(8,128)S(1)} custom-call(f32[1,128,128]{2,1,0:T(8,128)S(1)} %fusion.83), custom_call_target="InvertDiagBlocksLowerTriangular" | custom-call | tf_op jit(solution)/shard_map/while/body/eval_jaxpr/jit(_solve_triangular)/triangular_solve | solution.py:27
  315.1 5.2 %collective-permute-done.1 = f32[64,256]{1,0:T(8,128)S(1)} collective-permute-done((f32[64,256]{1,0:T(8,128)S(1)}, f32[64,256]{1,0:T(8,128)S(1)}, u32[]{:S(2)}, u32[]{:S(2)}) %collective-permute-start.1) | collective-permute-done | bytes 65568 | tf_op jit(solution)/shard_map/while/body/eval_jaxpr/ppermute | solution.py:21
  (183 shorter events, 54.3 us)
Async XLA Ops:
  1.9 10.8 %copy-start.2 = (f32[128,256]{1,0:T(8,128)S(1)}, f32[128,256]{1,0:T(8,128)}, u32[]{:S(2)}) copy-start(f32[128,256]{1,0:T(8,128)} %param.6) | copy-start | bytes 393220
  55.7 6.4 %collective-permute-start.1 = (f32[64,256]{1,0:T(8,128)S(1)}, f32[64,256]{1,0:T(8,128)S(1)}, u32[]{:S(2)}, u32[]{:S(2)}) collective-permute-start(f32[64,256]{1,0:T(8,128)S(1)} %get-tuple-element.90), channel_id=1, source_target_pairs={{30,0},{0,2},{2,4},{4,6},{6,8},{8,10},{10,12},{12,14},{14,16},{16,... | collective-permute-start | bytes 196616 | tf_op jit(solution)/shard_map/while/body/eval_jaxpr/ppermute | solution.py:21
  56.3 7.7 %collective-permute-start = (f32[64,640]{1,0:T(8,128)S(1)}, f32[64,640]{1,0:T(8,128)S(1)}, u32[]{:S(2)}, u32[]{:S(2)}) collective-permute-start(f32[64,640]{1,0:T(8,128)S(1)} %get-tuple-element.88), channel_id=1, source_target_pairs={{30,0},{0,2},{2,4},{4,6},{6,8},{8,10},{10,12},{12,14},{14,16},{16,... | collective-permute-start | bytes 491528 | tf_op jit(solution)/shard_map/while/body/eval_jaxpr/ppermute | solution.py:21
  58.4 6.0 %collective-permute-start.2 = (f32[64,64]{1,0:T(8,128)S(1)}, f32[64,64]{1,0:T(8,128)S(1)}, u32[]{:S(2)}, u32[]{:S(2)}) collective-permute-start(f32[64,64]{1,0:T(8,128)S(1)} %get-tuple-element.93), channel_id=1, source_target_pairs={{30,0},{0,2},{2,4},{4,6},{6,8},{8,10},{10,12},{12,14},{14,16},{16,... | collective-permute-start | bytes 49160 | tf_op jit(solution)/shard_map/while/body/eval_jaxpr/ppermute | solution.py:21
  107.5 6.4 %collective-permute-start.1 = (f32[64,256]{1,0:T(8,128)S(1)}, f32[64,256]{1,0:T(8,128)S(1)}, u32[]{:S(2)}, u32[]{:S(2)}) collective-permute-start(f32[64,256]{1,0:T(8,128)S(1)} %get-tuple-element.90), channel_id=1, source_target_pairs={{30,0},{0,2},{2,4},{4,6},{6,8},{8,10},{10,12},{12,14},{14,16},{16,... | collective-permute-start | bytes 196616 | tf_op jit(solution)/shard_map/while/body/eval_jaxpr/ppermute | solution.py:21
  108.0 7.7 %collective-permute-start = (f32[64,640]{1,0:T(8,128)S(1)}, f32[64,640]{1,0:T(8,128)S(1)}, u32[]{:S(2)}, u32[]{:S(2)}) collective-permute-start(f32[64,640]{1,0:T(8,128)S(1)} %get-tuple-element.88), channel_id=1, source_target_pairs={{30,0},{0,2},{2,4},{4,6},{6,8},{8,10},{10,12},{12,14},{14,16},{16,... | collective-permute-start | bytes 491528 | tf_op jit(solution)/shard_map/while/body/eval_jaxpr/ppermute | solution.py:21
  108.7 7.4 %collective-permute-start.2 = (f32[64,64]{1,0:T(8,128)S(1)}, f32[64,64]{1,0:T(8,128)S(1)}, u32[]{:S(2)}, u32[]{:S(2)}) collective-permute-start(f32[64,64]{1,0:T(8,128)S(1)} %get-tuple-element.93), channel_id=1, source_target_pairs={{30,0},{0,2},{2,4},{4,6},{6,8},{8,10},{10,12},{12,14},{14,16},{16,... | collective-permute-start | bytes 49160 | tf_op jit(solution)/shard_map/while/body/eval_jaxpr/ppermute | solution.py:21
  159.1 6.4 %collective-permute-start.1 = (f32[64,256]{1,0:T(8,128)S(1)}, f32[64,256]{1,0:T(8,128)S(1)}, u32[]{:S(2)}, u32[]{:S(2)}) collective-permute-start(f32[64,256]{1,0:T(8,128)S(1)} %get-tuple-element.90), channel_id=1, source_target_pairs={{30,0},{0,2},{2,4},{4,6},{6,8},{8,10},{10,12},{12,14},{14,16},{16,... | collective-permute-start | bytes 196616 | tf_op jit(solution)/shard_map/while/body/eval_jaxpr/ppermute | solution.py:21
  159.6 7.7 %collective-permute-start = (f32[64,640]{1,0:T(8,128)S(1)}, f32[64,640]{1,0:T(8,128)S(1)}, u32[]{:S(2)}, u32[]{:S(2)}) collective-permute-start(f32[64,640]{1,0:T(8,128)S(1)} %get-tuple-element.88), channel_id=1, source_target_pairs={{30,0},{0,2},{2,4},{4,6},{6,8},{8,10},{10,12},{12,14},{14,16},{16,... | collective-permute-start | bytes 491528 | tf_op jit(solution)/shard_map/while/body/eval_jaxpr/ppermute | solution.py:21
  160.3 7.4 %collective-permute-start.2 = (f32[64,64]{1,0:T(8,128)S(1)}, f32[64,64]{1,0:T(8,128)S(1)}, u32[]{:S(2)}, u32[]{:S(2)}) collective-permute-start(f32[64,64]{1,0:T(8,128)S(1)} %get-tuple-element.93), channel_id=1, source_target_pairs={{30,0},{0,2},{2,4},{4,6},{6,8},{8,10},{10,12},{12,14},{14,16},{16,... | collective-permute-start | bytes 49160 | tf_op jit(solution)/shard_map/while/body/eval_jaxpr/ppermute | solution.py:21
  210.7 6.4 %collective-permute-start.1 = (f32[64,256]{1,0:T(8,128)S(1)}, f32[64,256]{1,0:T(8,128)S(1)}, u32[]{:S(2)}, u32[]{:S(2)}) collective-permute-start(f32[64,256]{1,0:T(8,128)S(1)} %get-tuple-element.90), channel_id=1, source_target_pairs={{30,0},{0,2},{2,4},{4,6},{6,8},{8,10},{10,12},{12,14},{14,16},{16,... | collective-permute-start | bytes 196616 | tf_op jit(solution)/shard_map/while/body/eval_jaxpr/ppermute | solution.py:21
  211.2 7.7 %collective-permute-start = (f32[64,640]{1,0:T(8,128)S(1)}, f32[64,640]{1,0:T(8,128)S(1)}, u32[]{:S(2)}, u32[]{:S(2)}) collective-permute-start(f32[64,640]{1,0:T(8,128)S(1)} %get-tuple-element.88), channel_id=1, source_target_pairs={{30,0},{0,2},{2,4},{4,6},{6,8},{8,10},{10,12},{12,14},{14,16},{16,... | collective-permute-start | bytes 491528 | tf_op jit(solution)/shard_map/while/body/eval_jaxpr/ppermute | solution.py:21
  211.9 7.4 %collective-permute-start.2 = (f32[64,64]{1,0:T(8,128)S(1)}, f32[64,64]{1,0:T(8,128)S(1)}, u32[]{:S(2)}, u32[]{:S(2)}) collective-permute-start(f32[64,64]{1,0:T(8,128)S(1)} %get-tuple-element.93), channel_id=1, source_target_pairs={{30,0},{0,2},{2,4},{4,6},{6,8},{8,10},{10,12},{12,14},{14,16},{16,... | collective-permute-start | bytes 49160 | tf_op jit(solution)/shard_map/while/body/eval_jaxpr/ppermute | solution.py:21
  262.3 6.4 %collective-permute-start.1 = (f32[64,256]{1,0:T(8,128)S(1)}, f32[64,256]{1,0:T(8,128)S(1)}, u32[]{:S(2)}, u32[]{:S(2)}) collective-permute-start(f32[64,256]{1,0:T(8,128)S(1)} %get-tuple-element.90), channel_id=1, source_target_pairs={{30,0},{0,2},{2,4},{4,6},{6,8},{8,10},{10,12},{12,14},{14,16},{16,... | collective-permute-start | bytes 196616 | tf_op jit(solution)/shard_map/while/body/eval_jaxpr/ppermute | solution.py:21
  262.8 7.7 %collective-permute-start = (f32[64,640]{1,0:T(8,128)S(1)}, f32[64,640]{1,0:T(8,128)S(1)}, u32[]{:S(2)}, u32[]{:S(2)}) collective-permute-start(f32[64,640]{1,0:T(8,128)S(1)} %get-tuple-element.88), channel_id=1, source_target_pairs={{30,0},{0,2},{2,4},{4,6},{6,8},{8,10},{10,12},{12,14},{14,16},{16,... | collective-permute-start | bytes 491528 | tf_op jit(solution)/shard_map/while/body/eval_jaxpr/ppermute | solution.py:21
  263.4 7.4 %collective-permute-start.2 = (f32[64,64]{1,0:T(8,128)S(1)}, f32[64,64]{1,0:T(8,128)S(1)}, u32[]{:S(2)}, u32[]{:S(2)}) collective-permute-start(f32[64,64]{1,0:T(8,128)S(1)} %get-tuple-element.93), channel_id=1, source_target_pairs={{30,0},{0,2},{2,4},{4,6},{6,8},{8,10},{10,12},{12,14},{14,16},{16,... | collective-permute-start | bytes 49160 | tf_op jit(solution)/shard_map/while/body/eval_jaxpr/ppermute | solution.py:21
  313.9 6.4 %collective-permute-start.1 = (f32[64,256]{1,0:T(8,128)S(1)}, f32[64,256]{1,0:T(8,128)S(1)}, u32[]{:S(2)}, u32[]{:S(2)}) collective-permute-start(f32[64,256]{1,0:T(8,128)S(1)} %get-tuple-element.90), channel_id=1, source_target_pairs={{30,0},{0,2},{2,4},{4,6},{6,8},{8,10},{10,12},{12,14},{14,16},{16,... | collective-permute-start | bytes 196616 | tf_op jit(solution)/shard_map/while/body/eval_jaxpr/ppermute | solution.py:21
  314.4 7.7 %collective-permute-start = (f32[64,640]{1,0:T(8,128)S(1)}, f32[64,640]{1,0:T(8,128)S(1)}, u32[]{:S(2)}, u32[]{:S(2)}) collective-permute-start(f32[64,640]{1,0:T(8,128)S(1)} %get-tuple-element.88), channel_id=1, source_target_pairs={{30,0},{0,2},{2,4},{4,6},{6,8},{8,10},{10,12},{12,14},{14,16},{16,... | collective-permute-start | bytes 491528 | tf_op jit(solution)/shard_map/while/body/eval_jaxpr/ppermute | solution.py:21
  315.0 7.4 %collective-permute-start.2 = (f32[64,64]{1,0:T(8,128)S(1)}, f32[64,64]{1,0:T(8,128)S(1)}, u32[]{:S(2)}, u32[]{:S(2)}) collective-permute-start(f32[64,64]{1,0:T(8,128)S(1)} %get-tuple-element.93), channel_id=1, source_target_pairs={{30,0},{0,2},{2,4},{4,6},{6,8},{8,10},{10,12},{12,14},{14,16},{16,... | collective-permute-start | bytes 49160 | tf_op jit(solution)/shard_map/while/body/eval_jaxpr/ppermute | solution.py:21
  322.4 0.7 copy-start
  322.4 0.8 copy-start.1
